TPU v7x, 32 devices: a whole 2x2x4 slice. The times are simulated.
32 devices in a mesh: movie: 16 (over z, y, x), user: 2 (over core).
Axes of the slice: x: 2, y: 2, z: 4, core: 2. Of those that a mesh axis runs over, the one named last changes fastest.
Arguments:
- movie_ids: int32 [128, 128], P(('movie', 'user')), may hold values from 0 to 17919, as said below
- ratings: int32 [128, 128], P(('movie', 'user')), may hold values from 0 to 4
- valid: int32 [128, 128], P(('movie', 'user')), may hold values from 0 to 1, as said below
- weights: bfloat16 [5, 17920, 1024], P(None, 'movie'), may hold values from -0.5 to 0.5
- vis_bias: float32 [5, 17920], P(None, 'movie'), may hold values from -5 to 260
- hid_bias: float32 [1024], replicated, may hold values from -5 to 5
Outputs:
- weight_grad: float32 [5, 17920, 1024], P(None, 'movie')
- visible_grad: float32 [5, 17920], P(None, 'movie')
- hidden_grad: float32 [1024], replicated
- positive_hidden: float32 [128, 1024], P(('movie', 'user'))
Inputs may be any that keep to these rules, and one draw needn't show every extreme that they name: `movie_ids`: movie ids within one user's block are distinct. Of the slots with valid 1 among the users of one device (4 consecutive users), at most 96 name movies of any one block of 1120 consecutive movie ids; in every draw some such block takes exactly 96 from the users of every device. Slots with valid 0 are padding and count nowhere.
All inputs are finite; a program needn't handle non-finite values.
Results may differ from a plain program's by a relative error of at most 0.0054.
Values may be sent and summed in bfloat16 or wider, within the bound.
No kernel may reach another device: no remote copies, remote signals or barrier semaphores. Data moves between devices by JAX's collectives and lax.ppermute only.
A program may use at most 128 MiB of HBM per device.

v0:
```python
import jax
import jax.numpy as jnp
from jax import lax
from jax.sharding import PartitionSpec as P


def reconstruct(hidden_rows, weight_table, bias_row, rated_mask, levels):
    group_rows = hidden_rows.shape[0]
    rating_logits = (
        lax.dot_general(
            hidden_rows, weight_table, (((1,), (1,)), ((), ())), preferred_element_type=jnp.float32
        )
        + bias_row[None, :]
    )
    shaped = rating_logits.reshape(group_rows, levels, -1)
    largest = jnp.max(shaped, axis=1, keepdims=True)
    exponent = jnp.exp(shaped - largest)
    softened = (exponent / jnp.sum(exponent, axis=1, keepdims=True)).astype(jnp.bfloat16)
    return (softened * rated_mask[:, None, :]).reshape(group_rows, -1)


def hidden_phase(visible, weight_table, hid_bias, local_users, device_index):
    combined = jnp.dot(visible, weight_table, preferred_element_type=jnp.float32)
    all_probs = jax.nn.sigmoid(hid_bias[None, :] + lax.psum(combined, "movie"))
    own_rows = lax.dynamic_slice_in_dim(all_probs, device_index * local_users, local_users, 0)
    return (own_rows, all_probs.astype(jnp.bfloat16))


def on_device(movie_ids, ratings, valid, weights, vis_bias, hid_bias):
    owners = lax.axis_size("movie")
    device_index = lax.axis_index("movie")
    local_users, slot_count = movie_ids.shape
    levels, local_movies, hidden = weights.shape
    columns = levels * local_movies
    group_rows = owners * local_users
    capacity = max(2, 3 * local_users * slot_count // owners)
    flat_ids = movie_ids.reshape(-1)
    owner_ids = flat_ids // local_movies
    column_ids = ratings.reshape(-1) * local_movies + flat_ids % local_movies
    user_ids = jnp.arange(local_users * slot_count, dtype=jnp.int32) // slot_count
    usable = valid.reshape(-1) == 1
    matches = (owner_ids[:, None] == jnp.arange(owners, dtype=jnp.int32)[None, :]) & usable[:, None]
    ranking = jnp.cumsum(matches.astype(jnp.int32), axis=0) - 1
    placed = jnp.sum(jnp.where(matches, ranking, 0), axis=1)
    target = jnp.where(usable, owner_ids, owners)
    user_slots = (
        jnp.zeros((owners, capacity), jnp.int32).at[target, placed].set(user_ids, mode="drop")
    )
    column_slots = (
        jnp.full((owners, capacity), -1, jnp.int32).at[target, placed].set(column_ids, mode="drop")
    )
    got_users, got_columns = (
        lax.all_to_all(user_slots, "movie", split_axis=0, concat_axis=0, tiled=True),
        lax.all_to_all(column_slots, "movie", split_axis=0, concat_axis=0, tiled=True),
    )
    user_hot = (got_users[:, :, None] == jnp.arange(local_users, dtype=jnp.int32)).astype(
        jnp.bfloat16
    )
    column_hot = (got_columns[:, :, None] == jnp.arange(columns, dtype=jnp.int32)).astype(
        jnp.bfloat16
    )
    shown = jnp.einsum("ncu,ncj->nuj", user_hot, column_hot, preferred_element_type=jnp.float32)
    shown = shown.reshape(group_rows, columns).astype(jnp.bfloat16)
    rated_mask = jnp.sum(shown.reshape(group_rows, levels, local_movies), axis=1)
    weight_table = weights.reshape(columns, hidden)
    positive_own, positive_group = hidden_phase(
        shown, weight_table, hid_bias, local_users, device_index
    )
    reconstructed_ratings = reconstruct(
        positive_group, weight_table, vis_bias.reshape(columns), rated_mask, levels
    )
    negative_own, negative_group = hidden_phase(
        reconstructed_ratings, weight_table, hid_bias, local_users, device_index
    )
    contract = (((0,), (0,)), ((), ()))
    weight_grad = lax.dot_general(
        shown, positive_group, contract, preferred_element_type=jnp.float32
    )
    weight_grad = weight_grad - lax.dot_general(
        reconstructed_ratings, negative_group, contract, preferred_element_type=jnp.float32
    )
    visible_grad = jnp.sum(shown.astype(jnp.float32), axis=0) - jnp.sum(
        reconstructed_ratings.astype(jnp.float32), axis=0
    )
    weight_grad, visible_grad = lax.psum((weight_grad, visible_grad), "user")
    hidden_grad = lax.psum(jnp.sum(positive_own - negative_own, axis=0), ("movie", "user"))
    return (
        weight_grad.reshape(levels, local_movies, hidden),
        visible_grad.reshape(levels, local_movies),
        hidden_grad,
        positive_own,
    )


def solution(mesh):
    in_specs = (
        P(("movie", "user"), None),
        P(("movie", "user"), None),
        P(("movie", "user"), None),
        P(None, "movie", None),
        P(None, "movie"),
        P(),
    )
    out_specs = (P(None, "movie", None), P(None, "movie"), P(), P(("movie", "user"), None))
    return jax.shard_map(
        on_device, mesh=mesh, in_specs=in_specs, out_specs=out_specs, check_vma=False
    )
```

profile of v0, /device:TPU:0, one launch (start us, length us, event | category | flops | bytes accessed | tf_op | source)
XLA Modules:
  0.0 498.8 jit_solution(16229236096760497218)
XLA Ops:
  10.7 1.2 reduce-window.6
  12.8 70.4 %scatter_fusion.1 = s32[16,96]{1,0:T(8,128)} fusion(s32[16,96]{1,0:T(8,128)} %broadcast_in_dim.15, s32[512]{0:T(512)S(1)} %bitcast.81, s32[512]{0:T(512)S(1)} %get-tuple-element.10), kind=kCustom, calls=%fused_computation.1 | custom fusion | bytes 10240 | tf_op jit(solution)/shard_map/scatter | solution.py:50
  83.2 8.4 %all-to-all-start.1 = ((s32[16,1,96]{2,1,0:T(1,128)}), s32[16,1,96]{2,1,0:T(1,128)S(1)}, u32[]{:S(2)}, u32[]{:S(2)}) async-start(s32[16,1,96]{2,1,0:T(1,128)} %bitcast.13), calls=%async_computation.1 | async-start | bytes 16384 | tf_op jit(solution)/shard_map/all_to_all | solution.py:54
  91.7 25.2 %scatter_fusion = s32[16,96]{1,0:T(8,128)S(1)} fusion(s32[16,96]{1,0:T(8,128)S(1)} %broadcast_in_dim.12, s32[512]{0:T(512)S(1)} %bitcast.82, s32[512]{0:T(512)S(1)} %add_select_fusion.1), kind=kCustom, calls=%fused_computation | custom fusion | bytes 10240 | tf_op jit(solution)/shard_map/scatter | solution.py:47
  116.9 14.0 %all_to_all.18 = s32[16,1,96]{2,1,0:T(1,128)S(1)} all-to-all(s32[16,1,96]{2,1,0:T(1,128)S(1)} %bitcast.75), channel_id=1, replica_groups=mesh['movie'=16,'user'=2] {'movie'}, dimensions={0} | all-to-all | bytes 12288 | tf_op jit(solution)/shard_map/all_to_all | solution.py:53
  130.9 6.6 %convert_reduce_fusion.1 = (f32[5600]{0:T(1024)S(1)}, bf16[16,4,5600]{2,1,0:T(4,128)(2,1)S(1)}) fusion(s32[16,96]{1,0:T(8,128)S(1)} %bitcast.85, s32[16,96]{1,0:T(8,128)S(1)} %bitcast.86), kind=kOutput, calls=%fused_computation.12 | convolution fusion | flops 78490144 | bytes 751488 | tf_op jit(solution)/shard_map/ncu,ncj->nuj/dot_general | solution.py:62
  137.8 7.3 %fusion.24 = f32[64,1024]{1,0:T(8,128)} fusion(bf16[64,5600]{1,0:T(8,128)(2,1)S(1)} %convert_element_type.42, bf16[5600,1024]{1,0:T(8,128)(2,1)} %bitcast.77), kind=kOutput, calls=%fused_computation.65 | convolution fusion | flops 734003200 | bytes 12447744 | tf_op jit(solution)/shard_map/dot_general | solution.py:23
  147.2 1.1 mul.26
  148.3 2.7 mul.27
  151.1 98.4 %all-reduce.4.cloned.1.call-done = f32[64,1024]{1,0:T(8,128)} async-done(((f32[64,1024]{1,0:T(8,128)}), f32[64,1024]{1,0:T(8,128)}) %all-reduce.4.cloned.1.call-update) | async-done | bytes 262160 | tf_op jit(solution)/shard_map/psum | solution.py:24
  250.5 11.1 %fusion.9 = f32[5600,1024]{1,0:T(8,128)} fusion(bf16[64,5600]{1,0:T(8,128)(2,1)} %copy-done.1, f32[64,1024]{1,0:T(8,128)S(1)} %add_divide_fusion.1), kind=kOutput, calls=%fused_computation.22 | convolution fusion | flops 734068736 | bytes 23916544 | tf_op jit(solution)/shard_map/dot_general | solution.py:76
  261.7 4.7 convolution_add_fusion
  266.4 1.9 reshape.182
  270.8 7.1 %convolution_bitcast_fusion = f32[64,1024]{1,0:T(8,128)} fusion(bf16[5,1120,1024]{2,1,0:T(8,128)(2,1)} %param.9, bf16[64,5,1120]{2,1,0:T(8,128)(2,1)S(1)} %fusion.4), kind=kOutput, calls=%fused_computation.15 | convolution fusion | flops 734003200 | bytes 12447744 | tf_op jit(solution)/shard_map/dot_general | solution.py:23
  278.3 1.6 sub.52
  280.0 1.6 div.54
  281.5 3.0 div.55
  284.5 3.0 convert_reduce_fusion
  287.5 97.3 %all-reduce.6.cloned.1.call-done = f32[64,1024]{1,0:T(8,128)} async-done(((f32[64,1024]{1,0:T(8,128)}), f32[64,1024]{1,0:T(8,128)}) %all-reduce.6.cloned.1.call-update) | async-done | bytes 262160 | tf_op jit(solution)/shard_map/psum | solution.py:24
  385.8 15.5 %convolution_subtract_fusion = f32[5600,1024]{1,0:T(8,128)} fusion(f32[5600,1024]{1,0:T(8,128)} %fusion.9, bf16[64,5600]{1,0:T(8,128)(2,1)} %get-tuple-element.7, f32[64,1024]{1,0:T(8,128)S(1)} %add_divide_fusion), kind=kOutput, calls=%fused_computation.5 | convolution fusion | flops 739803136 | bytes 46854144 | tf_op jit(solution)/shard_map/dot_general | solution.py:79
  401.4 4.0 psum.38
  406.1 39.4 %psum.39 = f32[1024]{0:T(1024)} all-reduce(f32[1024]{0:T(1024)S(1)} %get-tuple-element.4), channel_id=1, replica_groups=mesh['movie'=16,'user'=2] {'movie','user'}, use_global_device_ids=true, to_apply=%region_15.16 | all-reduce | flops 1024 | bytes 8192 | tf_op jit(solution)/shard_map/psum | solution.py:86
  445.4 30.3 %all-reduce.8.cloned.1.call-done = f32[5,1120,1024]{2,1,0:T(8,128)} async-done(((f32[5,1120,1024]{2,1,0:T(8,128)}), f32[5,1120,1024]{2,1,0:T(8,128)}) %all-reduce.8.cloned.1.call-update) | async-done | bytes 22937616 | tf_op jit(solution)/shard_map/psum | solution.py:85
  475.8 16.5 %copy.37 = f32[5,1120,1024]{2,1,0:T(8,128)} copy(f32[5,1120,1024]{2,1,0:T(8,128)} %all-reduce.8.cloned.1.call-done) | data formatting | bytes 45875200
  (51 shorter events, 12.5 us)
Async XLA Ops:
  83.2 33.7 %all-to-all-start.1 = ((s32[16,1,96]{2,1,0:T(1,128)}), s32[16,1,96]{2,1,0:T(1,128)S(1)}, u32[]{:S(2)}, u32[]{:S(2)}) async-start(s32[16,1,96]{2,1,0:T(1,128)} %bitcast.13), calls=%async_computation.1 | async-start | bytes 16384 | tf_op jit(solution)/shard_map/all_to_all | solution.py:54
  91.6 157.9 %all-reduce.4.cloned.1.call-start = ((), (), s32[]{:S(2)}) async-start(), calls=%async_computation.2 | async-start | bytes 524288 | tf_op jit(solution)/shard_map/psum | solution.py:24
  137.8 7.4 %copy-start.1 = (bf16[64,5600]{1,0:T(8,128)(2,1)}, bf16[64,5600]{1,0:T(8,128)(2,1)S(1)}, u32[]{:S(2)}) copy-start(bf16[64,5600]{1,0:T(8,128)(2,1)S(1)} %convert_element_type.42) | copy-start | bytes 2150404
  137.8 7.6 %copy-start.3 = (f32[5,1120]{1,0:T(8,128)S(1)}, f32[5,1120]{1,0:T(8,128)}, u32[]{:S(2)}) copy-start(f32[5,1120]{1,0:T(8,128)} %param.10) | copy-start | bytes 67204
  145.2 239.6 %all-reduce.6.cloned.1.call-start = ((), (), s32[]{:S(2)}) async-start(), calls=%async_computation.3 | async-start | bytes 524288 | tf_op jit(solution)/shard_map/psum | solution.py:24
  146.4 103.1 %copy-start.4 = (f32[1024]{0:T(1024)S(1)}, f32[1024]{0:T(1024)}, u32[]{:S(2)}) copy-start(f32[1024]{0:T(1024)} %param.11) | copy-start | bytes 12292
  148.3 113.3 %slice-start = ((s8[11468800]{0:T(1024)(128)(4,1)}), s8[3080192]{0:T(1024)(128)(4,1)S(1)}, s32[]{:S(2)}) async-start(s8[11468800]{0:T(1024)(128)(4,1)} %bitcast.78), calls=%async_computation.5 | async-start | bytes 6160384
  250.5 11.2 %slice-start.1 = ((s8[11468800]{0:T(1024)(128)(4,1)}), s8[4194304]{0:T(1024)(128)(4,1)S(1)}, s32[]{:S(2)}) async-start(s8[11468800]{0:T(1024)(128)(4,1)} %bitcast.78), calls=%async_computation.6 | async-start | bytes 8388608
  250.5 11.2 %slice-start.2 = ((s8[11468800]{0:T(1024)(128)(4,1)}), s8[4194304]{0:T(1024)(128)(4,1)S(1)}, s32[]{:S(2)}) async-start(s8[11468800]{0:T(1024)(128)(4,1)} %bitcast.78), calls=%async_computation.7 | async-start | bytes 8388608
  277.9 197.9 %all-reduce.8.cloned.1.call-start = ((), (), s32[]{:S(2)}) async-start(), calls=%async_computation.4 | async-start | bytes 45875200 | tf_op jit(solution)/shard_map/psum | solution.py:85
  281.5 3.0 copy-start
  281.5 3.0 copy-start.2
Sparse Core Ops, SparseCore 0:
  145.3 104.1 all-reduce.3
  278.0 106.6 all-reduce.5
  401.4 74.2 all-reduce.7
where the time goes:
time: 501 us; the launch traced here: 499 us
  waiting for transfers between devices  226 us (45%)
  local copies, waits for them, and re-layouts  126 us (25%)
  blocking collectives  57.4 us (11%)
  matrix products  52.3 us (10%)
  between operations  14 us (3%)
  other arithmetic  13.7 us (3%)
  starting transfers between devices  8.93 us (2%)
    psum x2, waiting for transfers between devices, hidden_phase(): all_probs = jax.nn.sigmoid(hid_bias[None, :] + lax.psum(combined, 'movie'))  196 us
    scatter x1, local copies, waits for them, and re-layouts, on_device(): jnp.full((owners, capacity), -1, jnp.int32).at[target, placed]  70.4 us
    psum x1, blocking collectives, on_device(): lax.psum(jnp.sum(positive_own - negative_own, axis=0), ('movie', 'user'))  39.4 us
    psum x1, waiting for transfers between devices, on_device(): weight_grad, visible_grad = lax.psum((weight_grad, visible_grad), 'user')  30.3 us
    scatter x1, local copies, waits for them, and re-layouts, on_device(): jnp.zeros((owners, capacity), jnp.int32).at[target, placed]  25.2 us
    unnamed x17, local copies, waits for them, and re-layouts  16.6 us
    dot_general x1, matrix products, on_device(): lax.dot_general(reconstructed_ratings, negative_group, contract, preferre...  15.5 us
    dot_general x2, matrix products, hidden_phase(): jnp.dot(visible, weight_table, preferred_element_type=jnp.float32)  14.4 us
  transfers between devices with their start and end apart: 4, of which 3 were waited for; matrix products, arithmetic and copies ran while one was open for 8% of the time, Pallas kernels for 0%

commit v1 on v0

--- a/solution.py
+++ b/solution.py
@@ -1,7 +1,17 @@
+import functools
 import jax
 import jax.numpy as jnp
 from jax import lax
 from jax.sharding import PartitionSpec as P
+
+
+def part_routes_all(x_in, mesh_name, row_axis):
+    for ix in (mesh_name, row_axis):
+        x_in = lax.psum(x_in, axis_name=ix)
+    return x_in
+
+
+_try_all_orders = functools.partial(part_routes_all, mesh_name="user", row_axis="movie")
 
 
 def reconstruct(hidden_rows, weight_table, bias_row, rated_mask, levels):
@@ -83,7 +93,7 @@
         reconstructed_ratings.astype(jnp.float32), axis=0
     )
     weight_grad, visible_grad = lax.psum((weight_grad, visible_grad), "user")
-    hidden_grad = lax.psum(jnp.sum(positive_own - negative_own, axis=0), ("movie", "user"))
+    hidden_grad = _try_all_orders(jnp.sum(positive_own - negative_own, axis=0))
     return (
         weight_grad.reshape(levels, local_movies, hidden),
         visible_grad.reshape(levels, local_movies),

time: 501 us -> 501 us (level)
  no operation moved by 1% of the time
where the time goes in v1:
time: 501 us; the launch traced here: 499 us
  waiting for transfers between devices  225 us (45%)
  local copies, waits for them, and re-layouts  126 us (25%)
  blocking collectives  58.4 us (12%)
  matrix products  52.3 us (10%)
  between operations  14 us (3%)
  other arithmetic  13.7 us (3%)
  starting transfers between devices  8.93 us (2%)
    psum x2, waiting for transfers between devices, hidden_phase(): all_probs = jax.nn.sigmoid(hid_bias[None, :] + lax.psum(combined, 'movie'))  196 us
    scatter x1, local copies, waits for them, and re-layouts, on_device(): jnp.full((owners, capacity), -1, jnp.int32).at[target, placed]  70.4 us
    psum x1, blocking collectives, part_routes_all(): x_in = lax.psum(x_in, axis_name=ix)  40.4 us
    psum x1, waiting for transfers between devices, on_device(): weight_grad, visible_grad = lax.psum((weight_grad, visible_grad), 'user')  29.4 us
    scatter x1, local copies, waits for them, and re-layouts, on_device(): jnp.zeros((owners, capacity), jnp.int32).at[target, placed]  25.2 us
    unnamed x17, local copies, waits for them, and re-layouts  16.6 us
    dot_general x1, matrix products, on_device(): lax.dot_general(reconstructed_ratings, negative_group, contract, preferre...  15.5 us
    dot_general x2, matrix products, hidden_phase(): jnp.dot(visible, weight_table, preferred_element_type=jnp.float32)  14.4 us
  transfers between devices with their start and end apart: 4, of which 3 were waited for; matrix products, arithmetic and copies ran while one was open for 8% of the time, Pallas kernels for 0%

profile of v1, /device:TPU:0, one launch (start us, length us, event | category | flops | bytes accessed | tf_op | source)
XLA Modules:
  0.0 498.8 jit_solution(11637472938053155691)
XLA Ops:
  10.7 1.2 reduce-window.6
  12.8 70.4 %scatter_fusion.1 = s32[16,96]{1,0:T(8,128)} fusion(s32[16,96]{1,0:T(8,128)} %broadcast_in_dim.15, s32[512]{0:T(512)S(1)} %bitcast.81, s32[512]{0:T(512)S(1)} %get-tuple-element.12), kind=kCustom, calls=%fused_computation.1 | custom fusion | bytes 10240 | tf_op jit(solution)/shard_map/scatter | solution.py:60
  83.2 8.4 %all-to-all-start.1 = ((s32[16,1,96]{2,1,0:T(1,128)}), s32[16,1,96]{2,1,0:T(1,128)S(1)}, u32[]{:S(2)}, u32[]{:S(2)}) async-start(s32[16,1,96]{2,1,0:T(1,128)} %bitcast.13), calls=%async_computation.1 | async-start | bytes 16384 | tf_op jit(solution)/shard_map/all_to_all | solution.py:64
  91.7 25.2 %scatter_fusion = s32[16,96]{1,0:T(8,128)S(1)} fusion(s32[16,96]{1,0:T(8,128)S(1)} %broadcast_in_dim.12, s32[512]{0:T(512)S(1)} %bitcast.82, s32[512]{0:T(512)S(1)} %add_select_fusion.1), kind=kCustom, calls=%fused_computation | custom fusion | bytes 10240 | tf_op jit(solution)/shard_map/scatter | solution.py:57
  116.9 14.0 %all_to_all.18 = s32[16,1,96]{2,1,0:T(1,128)S(1)} all-to-all(s32[16,1,96]{2,1,0:T(1,128)S(1)} %bitcast.75), channel_id=1, replica_groups=mesh['movie'=16,'user'=2] {'movie'}, dimensions={0} | all-to-all | bytes 12288 | tf_op jit(solution)/shard_map/all_to_all | solution.py:63
  130.9 6.6 %convert_reduce_fusion.1 = (f32[5600]{0:T(1024)S(1)}, bf16[16,4,5600]{2,1,0:T(4,128)(2,1)S(1)}) fusion(s32[16,96]{1,0:T(8,128)S(1)} %bitcast.85, s32[16,96]{1,0:T(8,128)S(1)} %bitcast.86), kind=kOutput, calls=%fused_computation.12 | convolution fusion | flops 78490144 | bytes 751488 | tf_op jit(solution)/shard_map/ncu,ncj->nuj/dot_general | solution.py:72
  137.8 7.3 %fusion.24 = f32[64,1024]{1,0:T(8,128)} fusion(bf16[64,5600]{1,0:T(8,128)(2,1)S(1)} %convert_element_type.42, bf16[5600,1024]{1,0:T(8,128)(2,1)} %bitcast.77), kind=kOutput, calls=%fused_computation.65 | convolution fusion | flops 734003200 | bytes 12447744 | tf_op jit(solution)/shard_map/dot_general | solution.py:33
  147.2 1.1 mul.26
  148.3 2.7 mul.27
  151.1 98.4 %all-reduce.5.cloned.1.call-done = f32[64,1024]{1,0:T(8,128)} async-done(((f32[64,1024]{1,0:T(8,128)}), f32[64,1024]{1,0:T(8,128)}) %all-reduce.5.cloned.1.call-update) | async-done | bytes 262160 | tf_op jit(solution)/shard_map/psum | solution.py:34
  250.5 11.1 %fusion.9 = f32[5600,1024]{1,0:T(8,128)} fusion(bf16[64,5600]{1,0:T(8,128)(2,1)} %copy-done.1, f32[64,1024]{1,0:T(8,128)S(1)} %add_divide_fusion.1), kind=kOutput, calls=%fused_computation.22 | convolution fusion | flops 734068736 | bytes 23916544 | tf_op jit(solution)/shard_map/dot_general | solution.py:86
  261.7 4.7 convolution_add_fusion
  266.4 1.9 reshape.182
  270.8 7.1 %convolution_bitcast_fusion = f32[64,1024]{1,0:T(8,128)} fusion(bf16[5,1120,1024]{2,1,0:T(8,128)(2,1)} %param.9, bf16[64,5,1120]{2,1,0:T(8,128)(2,1)S(1)} %fusion.4), kind=kOutput, calls=%fused_computation.15 | convolution fusion | flops 734003200 | bytes 12447744 | tf_op jit(solution)/shard_map/dot_general | solution.py:33
  278.3 1.6 sub.52
  280.0 1.6 div.54
  281.5 3.0 div.55
  284.5 3.0 convert_reduce_fusion
  287.5 97.3 %all-reduce.7.cloned.1.call-done = f32[64,1024]{1,0:T(8,128)} async-done(((f32[64,1024]{1,0:T(8,128)}), f32[64,1024]{1,0:T(8,128)}) %all-reduce.7.cloned.1.call-update) | async-done | bytes 262160 | tf_op jit(solution)/shard_map/psum | solution.py:34
  385.8 15.5 %convolution_subtract_fusion = f32[5600,1024]{1,0:T(8,128)} fusion(f32[5600,1024]{1,0:T(8,128)} %fusion.9, bf16[64,5600]{1,0:T(8,128)(2,1)} %get-tuple-element.9, f32[64,1024]{1,0:T(8,128)S(1)} %add_divide_fusion), kind=kOutput, calls=%fused_computation.5 | convolution fusion | flops 739803136 | bytes 46854144 | tf_op jit(solution)/shard_map/dot_general | solution.py:89
  402.0 4.0 all-reduce
  406.1 40.4 %psum.47 = f32[1024]{0:T(1024)} all-reduce(f32[1024]{0:T(1024)S(1)} %get-tuple-element.5), channel_id=1, replica_groups=mesh['movie'=16,'user'=2] {'movie'}, use_global_device_ids=true, to_apply=%region_16.17 | all-reduce | flops 1024 | bytes 8192 | tf_op jit(solution)/shard_map/psum | solution.py:10
  446.4 29.4 %all-reduce.9.cloned.1.call-done = f32[5,1120,1024]{2,1,0:T(8,128)} async-done(((f32[5,1120,1024]{2,1,0:T(8,128)}), f32[5,1120,1024]{2,1,0:T(8,128)}) %all-reduce.9.cloned.1.call-update) | async-done | bytes 22937616 | tf_op jit(solution)/shard_map/psum | solution.py:95
  475.8 16.5 %copy.37 = f32[5,1120,1024]{2,1,0:T(8,128)} copy(f32[5,1120,1024]{2,1,0:T(8,128)} %all-reduce.9.cloned.1.call-done) | data formatting | bytes 45875200
  (51 shorter events, 12.5 us)
Async XLA Ops:
  83.2 33.7 %all-to-all-start.1 = ((s32[16,1,96]{2,1,0:T(1,128)}), s32[16,1,96]{2,1,0:T(1,128)S(1)}, u32[]{:S(2)}, u32[]{:S(2)}) async-start(s32[16,1,96]{2,1,0:T(1,128)} %bitcast.13), calls=%async_computation.1 | async-start | bytes 16384 | tf_op jit(solution)/shard_map/all_to_all | solution.py:64
  91.6 157.9 %all-reduce.5.cloned.1.call-start = ((), (), s32[]{:S(2)}) async-start(), calls=%async_computation.2 | async-start | bytes 524288 | tf_op jit(solution)/shard_map/psum | solution.py:34
  137.8 7.4 %copy-start.1 = (bf16[64,5600]{1,0:T(8,128)(2,1)}, bf16[64,5600]{1,0:T(8,128)(2,1)S(1)}, u32[]{:S(2)}) copy-start(bf16[64,5600]{1,0:T(8,128)(2,1)S(1)} %convert_element_type.42) | copy-start | bytes 2150404
  137.8 7.6 %copy-start.3 = (f32[5,1120]{1,0:T(8,128)S(1)}, f32[5,1120]{1,0:T(8,128)}, u32[]{:S(2)}) copy-start(f32[5,1120]{1,0:T(8,128)} %param.10) | copy-start | bytes 67204
  145.2 239.6 %all-reduce.7.cloned.1.call-start = ((), (), s32[]{:S(2)}) async-start(), calls=%async_computation.3 | async-start | bytes 524288 | tf_op jit(solution)/shard_map/psum | solution.py:34
  146.4 103.1 %copy-start.4 = (f32[1024]{0:T(1024)S(1)}, f32[1024]{0:T(1024)}, u32[]{:S(2)}) copy-start(f32[1024]{0:T(1024)} %param.11) | copy-start | bytes 12292
  148.3 113.3 %slice-start = ((s8[11468800]{0:T(1024)(128)(4,1)}), s8[3080192]{0:T(1024)(128)(4,1)S(1)}, s32[]{:S(2)}) async-start(s8[11468800]{0:T(1024)(128)(4,1)} %bitcast.78), calls=%async_computation.5 | async-start | bytes 6160384
  250.5 11.2 %slice-start.1 = ((s8[11468800]{0:T(1024)(128)(4,1)}), s8[4194304]{0:T(1024)(128)(4,1)S(1)}, s32[]{:S(2)}) async-start(s8[11468800]{0:T(1024)(128)(4,1)} %bitcast.78), calls=%async_computation.6 | async-start | bytes 8388608
  250.5 11.2 %slice-start.2 = ((s8[11468800]{0:T(1024)(128)(4,1)}), s8[4194304]{0:T(1024)(128)(4,1)S(1)}, s32[]{:S(2)}) async-start(s8[11468800]{0:T(1024)(128)(4,1)} %bitcast.78), calls=%async_computation.7 | async-start | bytes 8388608
  277.9 197.9 %all-reduce.9.cloned.1.call-start = ((), (), s32[]{:S(2)}) async-start(), calls=%async_computation.4 | async-start | bytes 45875200 | tf_op jit(solution)/shard_map/psum | solution.py:95
  281.5 3.0 copy-start
  281.5 3.0 copy-start.2
Sparse Core Ops, SparseCore 0:
  145.3 104.1 all-reduce.4
  278.0 106.6 all-reduce.6
  401.4 74.3 all-reduce.8
